TPU v7x, 32 devices: a whole 2x2x4 slice. The times are simulated.
32 devices in a mesh: gx: 2 (over y), gy: 4 (over x, core), gz: 4 (over z).
Axes of the slice: x: 2, y: 2, z: 4, core: 2. Of those that a mesh axis runs over, the one named last changes fastest.
Arguments:
- halo_position: float32 [3, 16, 16, 8, 128], P(None, 'gx', 'gy', 'gz'), may hold values from 0 to 1
- halo_velocity: float32 [3, 16, 16, 8, 128], P(None, 'gx', 'gy', 'gz'), may hold values from -1 to 1
- halo_mass: float32 [16, 16, 8, 128], P('gx', 'gy', 'gz'), may hold values from 0.005 to 0.08
- cell_counts: int32 [16, 16, 8], P('gx', 'gy', 'gz'), may hold values from 1 to 128, as said below
Outputs:
- predicted: float32 [3, 16, 16, 8, 128], P(None, 'gx', 'gy', 'gz')
Inputs may be any that keep to these rules, and one draw needn't show every extreme that they name: `cell_counts`: slots of a cell from its count on hold no halo.
All inputs are finite; a program needn't handle non-finite values.
Results may differ from a plain program's by a relative error of at most 0.0001.
Values sent between devices are 32-bit elements; how exact they have to be, the bound alone decides.
No kernel may reach another device: no remote copies, remote signals or barrier semaphores. Data moves between devices by JAX's collectives and lax.ppermute only.
A program may use at most 64 MiB of HBM per device.

v0:
```python
import jax
import jax.numpy as jnp
from jax import lax
from jax.sharding import PartitionSpec as P

soft_sq = 0.01
cut_sq = 0.64
cell_cap = 64


def extended_2(cells, sides, width):
    for axis, dim in sides:
        count = lax.axis_size(axis)
        head = lax.slice_in_dim(cells, 0, width, axis=dim)
        tail = lax.slice_in_dim(cells, cells.shape[dim] - width, cells.shape[dim], axis=dim)
        cells = jnp.concatenate(
            [
                lax.ppermute(tail, axis, [(i, (i + 1) % count) for i in range(count)]),
                cells,
                lax.ppermute(head, axis, [((i + 1) % count, i) for i in range(count)]),
            ],
            axis=dim,
        )
    return cells


def pull_block(extended, targets):
    depth_x, depth_y, depth_z, slot_count = targets.shape[1:]
    running = jnp.zeros(targets.shape, jnp.float32)
    for offset_code in range(27):
        shift_x = offset_code // 9
        shift_y = offset_code // 3 % 3
        shift_z = offset_code % 3
        sources = extended[
            :,
            shift_x : shift_x + depth_x,
            shift_y : shift_y + depth_y,
            shift_z : shift_z + depth_z,
            :,
        ]
        delta_x = (sources[0] + float(shift_x - 1))[..., :, None] - targets[0][..., None, :]
        delta_y = (sources[1] + float(shift_y - 1))[..., :, None] - targets[1][..., None, :]
        delta_z = (sources[2] + float(shift_z - 1))[..., :, None] - targets[2][..., None, :]
        dist_sq = delta_x * delta_x + delta_y * delta_y + delta_z * delta_z
        inv_dist = lax.rsqrt(dist_sq + soft_sq)
        tapering = jnp.maximum(1.0 - dist_sq / cut_sq, 0.0)
        weights = (
            sources[3][..., :, None] * (inv_dist * inv_dist * inv_dist) * (tapering * tapering)
        )
        running = running + jnp.stack(
            [
                jnp.sum(weights * delta_x, axis=-2),
                jnp.sum(weights * delta_y, axis=-2),
                jnp.sum(weights * delta_z, axis=-2),
            ],
            axis=0,
        )
    return running


def pull_field(extended):
    depth_x = extended.shape[1] - 2
    depth_y = extended.shape[2] - 2
    depth_z = extended.shape[3] - 2
    group_rows = 1
    for candidate in range(1, depth_x + 1):
        if depth_x % candidate == 0 and candidate * depth_y * depth_z <= cell_cap:
            group_rows = candidate
    targets = extended[:3, 1 : group_rows + 1, 1 : depth_y + 1, 1 : depth_z + 1]
    pieces = pull_block(extended, targets)
    return pieces


def body(halo_position, halo_velocity, halo_mass, cell_counts):
    occupied = lax.broadcasted_iota(jnp.int32, halo_mass.shape, 3) < cell_counts[..., None]
    held_mass = jnp.where(occupied, halo_mass, 0.0)
    outgoing = jnp.concatenate([halo_position, held_mass[None]], axis=0)
    mass_rim = None
    first_pull = None
    second_pull = None
    for round_index in range(2):
        widened = extended_2(outgoing, (("gx", 1),), 1)
        widened = extended_2(widened, (("gy", 2),), 1)
        widened = extended_2(widened, (("gz", 3),), 1)
        if round_index == 0:
            mass_rim = widened[3:4]
            first_pull = pull_field(widened)
            outgoing = halo_position + halo_velocity + 0.5 * first_pull
        else:
            second_pull = pull_field(jnp.concatenate([widened, mass_rim], axis=0))
    predicted = halo_position + halo_velocity + first_pull / 3.0 + second_pull / 6.0
    return jnp.where(occupied[None], predicted, 0.0)


def solution(mesh):
    return jax.shard_map(
        body,
        mesh=mesh,
        in_specs=(
            P(None, "gx", "gy", "gz", None),
            P(None, "gx", "gy", "gz", None),
            P("gx", "gy", "gz", None),
            P("gx", "gy", "gz"),
        ),
        out_specs=P(None, "gx", "gy", "gz", None),
        check_vma=False,
    )
```

profile of v0, /device:TPU:21, one launch (start us, length us, event | category | flops | bytes accessed | tf_op | source)
XLA Modules:
  0.0 321.5 jit_solution(9159901370591690055)
XLA Ops:
  0.0 0.8 copy.6
  0.8 0.9 fusion.862
  1.7 0.7 pad_maximum_fusion.20
  2.4 0.3 collective-permute-start
  2.7 1.2 collective-permute-start.1
  4.0 0.9 broadcast_select_fusion.1
  4.8 0.3 collective-permute-done
  5.1 0.2 collective-permute-done.1
  5.3 0.8 pad_maximum_fusion.9
  6.1 3.3 %collective-permute-start.2 = (f32[4,10,1,2,128]{4,3,2,1,0:T(2,128)S(1)}, f32[4,10,1,2,128]{4,3,2,1,0:T(2,128)S(1)}, u32[]{:S(2)}, u32[]{:S(2)}) collective-permute-start(f32[4,10,1,2,128]{4,3,2,1,0:T(2,128)S(1)} %get-tuple-element.449), channel_id=1, source_target_pairs={{0,4},{4,8},{8,12},{12,0},{1,5},{5,9},{9,13},{13,1},{2,6},{6,10},{... | collective-permute-start | bytes 122888 | tf_op jit(solution)/shard_map/ppermute | solution.py:18
  9.5 0.9 collective-permute-done.2
  10.5 2.3 collective-permute-done.3
  13.1 0.2 collective-permute-start.5
  13.3 1.3 collective-permute-start.4
  15.0 2.9 collective-permute-done.5
  17.9 2.8 collective-permute-done.4
  20.7 0.4 pad_maximum_fusion
  21.1 0.3 fusion.838
  21.3 0.3 slice_bitcast_fusion.55
  22.0 16.2 %fusion.80 = (f32[8,4,2,128]{3,2,1,0:T(2,128)S(1)}, f32[8,4,2,128]{3,2,1,0:T(2,128)S(1)}, f32[8,4,2,128]{3,2,1,0:T(2,128)S(1)}, f32[8,4,2,128]{3,2,1,0:T(2,128)S...) fusion(f32[8,4,2,128]{3,2,1,0:T(2,128)S(1)} %get-tuple-element., ...), kind=kLoop, calls=%fused_computation.458 | loop fusion | flops 72278016 | bytes 688128 | tf_op jit(solution)/shard_map/reduce_sum | solution.py:52
  38.2 20.4 %fusion.2 = (f32[8,4,2,128]{3,2,1,0:T(2,128)S(1)}, f32[8,4,2,128]{3,2,1,0:T(2,128)S(1)}, f32[8,4,2,128]{3,2,1,0:T(2,128)S(1)}, f32[8,4,2,128]{3,2,1,0:T(2,128)S(...) fusion(f32[8,4,2,128]{3,2,1,0:T(2,128)S(1)} %get-tuple-element., ...), kind=kLoop, calls=%fused_computation.380 | loop fusion | flops 96370688 | bytes 1015808 | tf_op jit(solution)/shard_map/reduce_sum | solution.py:52
  58.6 20.4 %fusion.41 = (f32[8,4,2,128]{3,2,1,0:T(2,128)S(1)}, f32[8,4,2,128]{3,2,1,0:T(2,128)S(1)}, f32[8,4,2,128]{3,2,1,0:T(2,128)S(1)}, f32[8,4,2,128]{3,2,1,0:T(2,128)S...) fusion(f32[8,4,2,128]{3,2,1,0:T(2,128)S(1)} %get-tuple-element., ...), kind=kLoop, calls=%fused_computation.419 | loop fusion | flops 96370688 | bytes 1015808 | tf_op jit(solution)/shard_map/reduce_sum | solution.py:52
  79.0 20.4 %fusion.28 = (f32[8,4,2,128]{3,2,1,0:T(2,128)S(1)}, f32[8,4,2,128]{3,2,1,0:T(2,128)S(1)}, f32[8,4,2,128]{3,2,1,0:T(2,128)S(1)}, f32[8,4,2,128]{3,2,1,0:T(2,128)S...) fusion(f32[8,4,2,128]{3,2,1,0:T(2,128)S(1)} %get-tuple-element., ...), kind=kLoop, calls=%fused_computation.406 | loop fusion | flops 96370688 | bytes 1015808 | tf_op jit(solution)/shard_map/reduce_sum | solution.py:52
  99.3 20.4 %fusion.15 = (f32[8,4,2,128]{3,2,1,0:T(2,128)S(1)}, f32[8,4,2,128]{3,2,1,0:T(2,128)S(1)}, f32[8,4,2,128]{3,2,1,0:T(2,128)S(1)}, f32[8,4,2,128]{3,2,1,0:T(2,128)S...) fusion(f32[8,4,2,128]{3,2,1,0:T(2,128)S(1)} %get-tuple-element., ...), kind=kLoop, calls=%fused_computation.393 | loop fusion | flops 96370688 | bytes 1015808 | tf_op jit(solution)/shard_map/reduce_sum | solution.py:52
  119.7 20.4 %fusion.54 = (f32[8,4,2,128]{3,2,1,0:T(2,128)S(1)}, f32[8,4,2,128]{3,2,1,0:T(2,128)S(1)}, f32[8,4,2,128]{3,2,1,0:T(2,128)S(1)}, f32[8,4,2,128]{3,2,1,0:T(2,128)S...) fusion(f32[8,4,2,128]{3,2,1,0:T(2,128)S(1)} %get-tuple-element., ...), kind=kLoop, calls=%fused_computation.432 | loop fusion | flops 96370688 | bytes 1015808 | tf_op jit(solution)/shard_map/reduce_sum | solution.py:52
  140.1 20.4 %fusion.67 = (f32[8,4,2,128]{3,2,1,0:T(2,128)S(1)}, f32[8,4,2,128]{3,2,1,0:T(2,128)S(1)}, f32[8,4,2,128]{3,2,1,0:T(2,128)S(1)}, f32[8,4,2,128]{3,2,1,0:T(2,128)S...) fusion(f32[8,4,2,128]{3,2,1,0:T(2,128)S(1)} %get-tuple-element., ...), kind=kLoop, calls=%fused_computation.445 | loop fusion | flops 96370688 | bytes 1015808 | tf_op jit(solution)/shard_map/reduce_sum | solution.py:52
  160.5 1.5 multiply_add_fusion
  162.1 1.3 collective-permute-start.6
  163.4 0.2 collective-permute-start.7
  163.7 1.0 collective-permute-done.6
  164.7 1.2 collective-permute-done.7
  166.0 2.7 collective-permute-start.8
  168.7 0.9 collective-permute-done.8
  169.7 2.3 collective-permute-done.9
  172.2 2.1 collective-permute-start.11
  174.6 1.9 collective-permute-done.11
  176.6 3.5 %collective-permute-done.10 = f32[3,10,6,1,128]{4,3,2,1,0:T(1,128)S(1)} collective-permute-done((f32[3,10,6,1,128]{4,3,2,1,0:T(1,128)S(1)}, f32[3,10,6,1,128]{4,3,2,1,0:T(1,128)S(1)}, u32[]{:S(2)}, u32[]{:S(2)}) %collective-permute-start.10) | collective-permute-done | bytes 92192 | tf_op jit(solution)/shard_map/ppermute | solution.py:18
  180.1 0.3 pad_maximum_fusion.1
  180.6 0.2 fusion.781
  180.8 0.3 fusion.782
  181.1 16.0 %fusion.431 = (f32[8,4,2,128]{3,2,1,0:T(2,128)S(1)}, f32[8,4,2,128]{3,2,1,0:T(2,128)S(1)}, f32[8,4,2,128]{3,2,1,0:T(2,128)S(1)}, f32[8,4,2,128]{3,2,1,0:T(2,128)...) fusion(f32[8,4,2,128]{3,2,1,0:T(2,128)S(1)} %get-tuple-element., ...), kind=kLoop, calls=%fused_computation.809 | loop fusion | flops 72278016 | bytes 688128 | tf_op jit(solution)/shard_map/reduce_sum | solution.py:52
  197.1 20.4 %fusion.392 = (f32[8,4,2,128]{3,2,1,0:T(2,128)S(1)}, f32[8,4,2,128]{3,2,1,0:T(2,128)S(1)}, f32[8,4,2,128]{3,2,1,0:T(2,128)S(1)}, f32[8,4,2,128]{3,2,1,0:T(2,128)...) fusion(f32[8,4,2,128]{3,2,1,0:T(2,128)S(1)} %get-tuple-element., ...), kind=kLoop, calls=%fused_computation.770 | loop fusion | flops 96370688 | bytes 1015808 | tf_op jit(solution)/shard_map/reduce_sum | solution.py:52
  217.5 20.4 %fusion.379 = (f32[8,4,2,128]{3,2,1,0:T(2,128)S(1)}, f32[8,4,2,128]{3,2,1,0:T(2,128)S(1)}, f32[8,4,2,128]{3,2,1,0:T(2,128)S(1)}, f32[8,4,2,128]{3,2,1,0:T(2,128)...) fusion(f32[8,4,2,128]{3,2,1,0:T(2,128)S(1)} %get-tuple-element., ...), kind=kLoop, calls=%fused_computation.757 | loop fusion | flops 96370688 | bytes 1015808 | tf_op jit(solution)/shard_map/reduce_sum | solution.py:52
  237.9 20.4 %fusion.366 = (f32[8,4,2,128]{3,2,1,0:T(2,128)S(1)}, f32[8,4,2,128]{3,2,1,0:T(2,128)S(1)}, f32[8,4,2,128]{3,2,1,0:T(2,128)S(1)}, f32[8,4,2,128]{3,2,1,0:T(2,128)...) fusion(f32[8,4,2,128]{3,2,1,0:T(2,128)S(1)} %get-tuple-element., ...), kind=kLoop, calls=%fused_computation.744 | loop fusion | flops 96370688 | bytes 1015808 | tf_op jit(solution)/shard_map/reduce_sum | solution.py:52
  258.3 20.4 %fusion.418 = (f32[8,4,2,128]{3,2,1,0:T(2,128)S(1)}, f32[8,4,2,128]{3,2,1,0:T(2,128)S(1)}, f32[8,4,2,128]{3,2,1,0:T(2,128)S(1)}, f32[8,4,2,128]{3,2,1,0:T(2,128)...) fusion(f32[8,4,2,128]{3,2,1,0:T(2,128)S(1)} %get-tuple-element., ...), kind=kLoop, calls=%fused_computation.796 | loop fusion | flops 96370688 | bytes 1015808 | tf_op jit(solution)/shard_map/reduce_sum | solution.py:52
  278.7 20.4 %fusion.353 = (f32[8,4,2,128]{3,2,1,0:T(2,128)S(1)}, f32[8,4,2,128]{3,2,1,0:T(2,128)S(1)}, f32[8,4,2,128]{3,2,1,0:T(2,128)S(1)}, f32[8,4,2,128]{3,2,1,0:T(2,128)...) fusion(f32[8,4,2,128]{3,2,1,0:T(2,128)S(1)} %get-tuple-element., ...), kind=kLoop, calls=%fused_computation.731 | loop fusion | flops 96370688 | bytes 1015808 | tf_op jit(solution)/shard_map/reduce_sum | solution.py:52
  299.1 20.4 %fusion.405 = (f32[8,4,2,128]{3,2,1,0:T(2,128)S(1)}, f32[8,4,2,128]{3,2,1,0:T(2,128)S(1)}, f32[8,4,2,128]{3,2,1,0:T(2,128)S(1)}, f32[8,4,2,128]{3,2,1,0:T(2,128)...) fusion(f32[8,4,2,128]{3,2,1,0:T(2,128)S(1)} %get-tuple-element., ...), kind=kLoop, calls=%fused_computation.783 | loop fusion | flops 96370688 | bytes 1015808 | tf_op jit(solution)/shard_map/reduce_sum | solution.py:52
  319.4 2.0 broadcast_select_fusion
  (25 shorter events, 2.1 us)
Async XLA Ops:
  0.0 9.4 %copy-start = (f32[3,8,4,2,128]{4,3,2,1,0:T(2,128)S(1)}, f32[3,8,4,2,128]{4,3,2,1,0:T(2,128)}, u32[]{:S(2)}) copy-start(f32[3,8,4,2,128]{4,3,2,1,0:T(2,128)} %param.4) | copy-start | bytes 294916
  2.4 2.7 collective-permute-start
  2.7 2.6 collective-permute-start.1
  6.1 4.4 %collective-permute-start.2 = (f32[4,10,1,2,128]{4,3,2,1,0:T(2,128)S(1)}, f32[4,10,1,2,128]{4,3,2,1,0:T(2,128)S(1)}, u32[]{:S(2)}, u32[]{:S(2)}) collective-permute-start(f32[4,10,1,2,128]{4,3,2,1,0:T(2,128)S(1)} %get-tuple-element.449), channel_id=1, source_target_pairs={{0,4},{4,8},{8,12},{12,0},{1,5},{5,9},{9,13},{13,1},{2,6},{6,10},{... | collective-permute-start | bytes 122888 | tf_op jit(solution)/shard_map/ppermute | solution.py:18
  9.4 3.4 %collective-permute-start.3 = (f32[4,10,1,2,128]{4,3,2,1,0:T(2,128)S(1)}, f32[4,10,1,2,128]{4,3,2,1,0:T(2,128)S(1)}, u32[]{:S(2)}, u32[]{:S(2)}) collective-permute-start(f32[4,10,1,2,128]{4,3,2,1,0:T(2,128)S(1)} %get-tuple-element.450), channel_id=1, source_target_pairs={{4,0},{8,4},{12,8},{0,12},{5,1},{9,5},{13,9},{1,13},{6,2},{10,6},{... | collective-permute-start | bytes 122888 | tf_op jit(solution)/shard_map/ppermute | solution.py:20
  13.1 4.8 %collective-permute-start.5 = (f32[4,10,6,1,128]{4,3,2,1,0:T(1,128)S(1)}, f32[4,10,6,1,128]{4,3,2,1,0:T(1,128)S(1)}, u32[]{:S(2)}, u32[]{:S(2)}) collective-permute-start(f32[4,10,6,1,128]{4,3,2,1,0:T(1,128)S(1)} %get-tuple-element.417), channel_id=1, source_target_pairs={{1,0},{2,1},{3,2},{0,3},{5,4},{6,5},{7,6},{4,7},{9,8},{10,9},{11,1... | collective-permute-start | bytes 368648 | tf_op jit(solution)/shard_map/ppermute | solution.py:20
  13.3 7.3 %collective-permute-start.4 = (f32[4,10,6,1,128]{4,3,2,1,0:T(1,128)S(1)}, f32[4,10,6,1,128]{4,3,2,1,0:T(1,128)S(1)}, u32[]{:S(2)}, u32[]{:S(2)}) collective-permute-start(f32[4,10,6,1,128]{4,3,2,1,0:T(1,128)S(1)} %get-tuple-element.418), channel_id=1, source_target_pairs={{0,1},{1,2},{2,3},{3,0},{4,5},{5,6},{6,7},{7,4},{8,9},{9,10},{10,1... | collective-permute-start | bytes 368648 | tf_op jit(solution)/shard_map/ppermute | solution.py:18
  140.1 20.4 %copy-start.1 = (f32[3,8,4,2,128]{4,3,2,1,0:T(2,128)S(1)}, f32[3,8,4,2,128]{4,3,2,1,0:T(2,128)}, u32[]{:S(2)}) copy-start(f32[3,8,4,2,128]{4,3,2,1,0:T(2,128)} %param.5) | copy-start | bytes 294916
  162.1 2.6 collective-permute-start.6
  163.4 2.5 collective-permute-start.7
  166.0 3.7 %collective-permute-start.8 = (f32[3,10,1,2,128]{4,3,2,1,0:T(2,128)S(1)}, f32[3,10,1,2,128]{4,3,2,1,0:T(2,128)S(1)}, u32[]{:S(2)}, u32[]{:S(2)}) collective-permute-start(f32[3,10,1,2,128]{4,3,2,1,0:T(2,128)S(1)} %get-tuple-element.481), channel_id=1, source_target_pairs={{0,4},{4,8},{8,12},{12,0},{1,5},{5,9},{9,13},{13,1},{2,6},{6,10},{... | collective-permute-start | bytes 92168 | tf_op jit(solution)/shard_map/ppermute | solution.py:18
  168.6 3.3 %collective-permute-start.9 = (f32[3,10,1,2,128]{4,3,2,1,0:T(2,128)S(1)}, f32[3,10,1,2,128]{4,3,2,1,0:T(2,128)S(1)}, u32[]{:S(2)}, u32[]{:S(2)}) collective-permute-start(f32[3,10,1,2,128]{4,3,2,1,0:T(2,128)S(1)} %get-tuple-element.482), channel_id=1, source_target_pairs={{4,0},{8,4},{12,8},{0,12},{5,1},{9,5},{13,9},{1,13},{6,2},{10,6},{... | collective-permute-start | bytes 92168 | tf_op jit(solution)/shard_map/ppermute | solution.py:20
  172.2 4.4 %collective-permute-start.11 = (f32[3,10,6,1,128]{4,3,2,1,0:T(1,128)S(1)}, f32[3,10,6,1,128]{4,3,2,1,0:T(1,128)S(1)}, u32[]{:S(2)}, u32[]{:S(2)}) collective-permute-start(f32[3,10,6,1,128]{4,3,2,1,0:T(1,128)S(1)} %get-tuple-element.445), channel_id=1, source_target_pairs={{1,0},{2,1},{3,2},{0,3},{5,4},{6,5},{7,6},{4,7},{9,8},{10,9},{11,1... | collective-permute-start | bytes 276488 | tf_op jit(solution)/shard_map/ppermute | solution.py:20
  174.3 5.8 %collective-permute-start.10 = (f32[3,10,6,1,128]{4,3,2,1,0:T(1,128)S(1)}, f32[3,10,6,1,128]{4,3,2,1,0:T(1,128)S(1)}, u32[]{:S(2)}, u32[]{:S(2)}) collective-permute-start(f32[3,10,6,1,128]{4,3,2,1,0:T(1,128)S(1)} %get-tuple-element.446), channel_id=1, source_target_pairs={{0,1},{1,2},{2,3},{3,0},{4,5},{5,6},{6,7},{7,4},{8,9},{9,10},{10,1... | collective-permute-start | bytes 276488 | tf_op jit(solution)/shard_map/ppermute | solution.py:18
where the time goes:
time: 325 us; the launch traced here: 321 us
  other arithmetic  287 us (88%)
  waiting for transfers between devices  20.3 us (6%)
  starting transfers between devices  12.6 us (4%)
    reduce_sum x14, other arithmetic, pull_block(): jnp.sum(weights * delta_x, axis=-2)  277 us
    ppermute x6, waiting for transfers between devices, extended_2(): lax.ppermute(head, axis, [((i + 1) % count, i) for i in range(count)])  10.9 us
    ppermute x6, waiting for transfers between devices, extended_2(): lax.ppermute(tail, axis, [(i, (i + 1) % count) for i in range(count)])  9.4 us
    ppermute x6, starting transfers between devices, extended_2(): lax.ppermute(tail, axis, [(i, (i + 1) % count) for i in range(count)])  8.81 us
  transfers between devices with their start and end apart: 12, of which 12 were waited for; matrix products, arithmetic and copies ran while one was open for 1% of the time, Pallas kernels for 0%

commit v1 on v0

v1 whole, which is shorter than its diff:
```python
import functools
import jax, jax.numpy as jnp
from jax import lax
from jax.sharding import PartitionSpec as P
from jax.experimental import pallas as pl
from jax.experimental.pallas import tpu as pltpu

soft_sq = 0.01
cut_sq = 0.64
f32, bf16 = jnp.float32, jnp.bfloat16


def rounded(v):
    return v.astype(bf16).astype(f32)


def split3(v):
    a = rounded(v)
    rest = v - a
    b = rounded(rest)
    return a, b, rest - b


def squares(v, extra=0.0):
    a = rounded(v)
    rest = v - a
    b = rounded(rest)
    top = a * a
    top_a = rounded(top)
    low = 2.0 * a * rest + rest * rest + extra
    la, lb, lc = split3(low)
    return (a, b, rest - b), (top_a, top - top_a, la, lb, lc)


def source_rows(v):
    (a, b, c), (pa, pb, pc, pd, pe) = squares(v)
    one = jnp.ones_like(v)
    return [a, one, one, pa, pb, a, b, b, a, c, one, one, one, pc, pd, pe]


def target_rows(v, extra):
    (a, b, c), (pa, pb, pc, pd, pe) = squares(v, extra)
    one = jnp.ones_like(v)
    return [-2.0 * a, pa, pb, one, one, -2.0 * b, -2.0 * a, -2.0 * b, -2.0 * c, -2.0 * a, pc, pd, pe, one, one, one]


def pull_kernel(grid, ext_ref, own_ref, out_ref, left, sums, right, rows):
    nx, ny, nz = grid
    ey, ez = ny + 2, nz + 2
    cells = ext_ref.shape[1]
    own = own_ref.shape[1]

    def prep_sources(i, _):
        at = pl.ds(pl.multiple_of(i * 8, 8), 8)
        where = 0
        for d in range(3):
            for piece in source_rows(ext_ref[d, at, :] - 0.5):
                rows[where * 8:where * 8 + 8, :] = piece
                where += 1
        mass = ext_ref[3, at, :] * (1.0 / (cut_sq * cut_sq))
        pieces = list(split3(mass))
        for d in range(3):
            pieces += list(split3(mass * (ext_ref[d, at, :] - 0.5)))
        for piece in pieces:
            rows[where * 8:where * 8 + 8, :] = piece
            where += 1
        for j in range(8):
            block = rows[pl.ds(j, 48, stride=8), :]
            left[i * 8 + j] = block.T.astype(bf16)
            block = rows[pl.ds(48 * 8 + j, 16, stride=8), :]
            sums[i * 8 + j] = block.astype(bf16)
        return 0

    rows[...] = jnp.zeros_like(rows)
    lax.fori_loop(0, cells // 8, prep_sources, 0)

    def prep_targets(i, _):
        at = pl.ds(pl.multiple_of(i * 8, 8), 8)
        for d in range(3):
            base = own_ref[d, at, :] - 0.5
            for o in range(3):
                for k, piece in enumerate(target_rows(base - float(o - 1), soft_sq if d == 2 else 0.0)):
                    rows[k * 8:k * 8 + 8, :] = piece
                for j in range(8):
                    block = rows[pl.ds(j, 16, stride=8), :]
                    right[i * 8 + j, d * 3 + o] = block.astype(bf16)
        return 0

    lax.fori_loop(0, own // 8, prep_targets, 0)

    def one_pair(p, _):
        tx = p // ny
        ty = p % ny
        for z0 in range(0, nz, 2):
            me = p * nz + z0
            acc = jnp.zeros((16, 256), f32)
            side = [jnp.zeros((8, 256), f32) for _ in range(3)]
            for ox in range(3):
                acc_x = jnp.zeros((16, 256), f32)
                for oy in range(3):
                    acc_y = jnp.zeros((16, 256), f32)
                    first = ((tx + ox) * ey + ty + oy) * ez + z0
                    both = [[jnp.concatenate([right[me + t, ox], right[me + t, 3 + oy], right[me + t, 6 + oz]], axis=0)
                             for oz in range(3)] for t in range(2)]
                    for layer in range(4):
                        part = []
                        if layer == 0:
                            rhs = both[0][0]
                        elif layer == 3:
                            rhs = both[1][2]
                        else:
                            rhs = jnp.concatenate([both[0][layer], both[1][layer - 1]], axis=1)
                        q = jnp.dot(left[first + layer], rhs, preferred_element_type=f32)
                        r = lax.rsqrt(q)
                        t = jnp.maximum((cut_sq + soft_sq) - q, 0.0)
                        t = r * t
                        w = t * t * r
                        hi = w.astype(bf16)
                        lo = (w - hi.astype(f32)).astype(bf16)
                        fe = sums[first + layer]
                        got = jnp.dot(jnp.concatenate([fe, fe], axis=1), jnp.concatenate([hi, lo], axis=0), preferred_element_type=f32)
                        if layer == 0:
                            got = jnp.concatenate([got, jnp.zeros_like(got)], axis=1)
                            zed = jnp.concatenate([-got[:8, :128], jnp.zeros((8, 128), f32)], axis=1)
                        elif layer == 3:
                            got = jnp.concatenate([jnp.zeros_like(got), got], axis=1)
                            zed = got[:8]
                        elif layer == 1:
                            zed = jnp.concatenate([jnp.zeros((8, 128), f32), -got[:8, 128:]], axis=1)
                        else:
                            zed = jnp.concatenate([got[:8, :128], jnp.zeros((8, 128), f32)], axis=1)
                        side[2] = side[2] + zed
                        acc_y = acc_y + got
                    if oy != 1:
                        side[1] = side[1] + float(oy - 1) * acc_y[:8]
                    acc_x = acc_x + acc_y
                if ox != 1:
                    side[0] = side[0] + float(ox - 1) * acc_x[:8]
                acc = acc + acc_x
            total = acc[0:1] + acc[1:2] + acc[2:3]
            for d in range(3):
                moment = acc[3 * d + 3:3 * d + 4] + acc[3 * d + 4:3 * d + 5] + acc[3 * d + 5:3 * d + 6]
                shift = side[d][0:1] + side[d][1:2] + side[d][2:3]
                for t in range(2):
                    lanes = slice(128 * t, 128 * t + 128)
                    at = own_ref[d, pl.ds(me + t, 1), :] - 0.5
                    out_ref[d, pl.ds(me + t, 1), :] = (moment[:, lanes] + shift[:, lanes]) - at * total[:, lanes]
        return 0

    lax.fori_loop(0, nx * ny, one_pair, 0)


def pull(ext, own, grid):
    cells = ext.shape[1]
    count = own.shape[1]
    return pl.pallas_call(
        functools.partial(pull_kernel, grid),
        out_shape=jax.ShapeDtypeStruct((3, count, 128), f32),
        in_specs=[pl.BlockSpec(memory_space=pltpu.VMEM)] * 2,
        out_specs=pl.BlockSpec(memory_space=pltpu.VMEM),
        scratch_shapes=[
            pltpu.VMEM((cells, 128, 48), bf16),
            pltpu.VMEM((cells, 16, 128), bf16),
            pltpu.VMEM((count, 9, 16, 128), bf16),
            pltpu.VMEM((64 * 8, 128), f32),
        ],
        compiler_params=pltpu.CompilerParams(vmem_limit_bytes=60 * 2**20),
    )(ext, own)


def extended_2(cells, sides, width):
    for axis, dim in sides:
        count = lax.axis_size(axis)
        head = lax.slice_in_dim(cells, 0, width, axis=dim)
        tail = lax.slice_in_dim(cells, cells.shape[dim] - width, cells.shape[dim], axis=dim)
        cells = jnp.concatenate(
            [
                lax.ppermute(tail, axis, [(i, (i + 1) % count) for i in range(count)]),
                cells,
                lax.ppermute(head, axis, [((i + 1) % count, i) for i in range(count)]),
            ],
            axis=dim,
        )
    return cells


def pull_field(extended, targets):
    slots = targets.shape[-1]
    flat = pull(extended.reshape(4, -1, slots), targets.reshape(3, -1, slots), targets.shape[1:4])
    return flat.reshape(targets.shape)


def body(halo_position, halo_velocity, halo_mass, cell_counts):
    occupied = lax.broadcasted_iota(jnp.int32, halo_mass.shape, 3) < cell_counts[..., None]
    held_mass = jnp.where(occupied, halo_mass, 0.0)
    outgoing = jnp.concatenate([halo_position, held_mass[None]], axis=0)
    mass_rim = None
    first_pull = None
    second_pull = None
    for round_index in range(2):
        widened = extended_2(outgoing, (("gx", 1),), 1)
        widened = extended_2(widened, (("gy", 2),), 1)
        widened = extended_2(widened, (("gz", 3),), 1)
        if round_index == 0:
            mass_rim = widened[3:4]
            first_pull = pull_field(widened, halo_position)
            outgoing = halo_position + halo_velocity + 0.5 * first_pull
        else:
            second_pull = pull_field(jnp.concatenate([widened, mass_rim], axis=0), outgoing)
    predicted = halo_position + halo_velocity + first_pull / 3.0 + second_pull / 6.0
    return jnp.where(occupied[None], predicted, 0.0)


def solution(mesh):
    return jax.shard_map(
        body,
        mesh=mesh,
        in_specs=(
            P(None, "gx", "gy", "gz", None),
            P(None, "gx", "gy", "gz", None),
            P("gx", "gy", "gz", None),
            P("gx", "gy", "gz"),
        ),
        out_specs=P(None, "gx", "gy", "gz", None),
        check_vma=False,
    )
```

time: 325 us -> 145 us (0.45)
  other arithmetic: 287 us -> 6.07 us
  Pallas kernels: 0 us -> 101 us
    reduce_sum x14 -> x0, other arithmetic: 277 us -> none  [pull_block(): jnp.sum(weights * delta_x, axis=-2)]
    pallas_call x0 -> x2, Pallas kernels: none -> 101 us  [pull(): pl.pallas_call(functools.partial(pull_kernel, grid), out_shape=jax.ShapeD...]
  transfers between devices with their start and end apart: 12 -> 12, of which waited for: 12 -> 11; matrix products, arithmetic and copies ran while one was open for 1% -> 1% of each run, Pallas kernels for 0% -> 0%
where the time goes in v1:
time: 145 us; the launch traced here: 143 us
  Pallas kernels  101 us (70%)
  waiting for transfers between devices  20.6 us (14%)
  starting transfers between devices  12.3 us (8%)
  other arithmetic  6.07 us (4%)
  local copies, waits for them, and re-layouts  2.11 us (1%)
    pallas_call x2, Pallas kernels, pull(): pl.pallas_call(functools.partial(pull_kernel, grid), out_shape=jax.ShapeD...  101 us
    ppermute x6, waiting for transfers between devices, extended_2(): lax.ppermute(tail, axis, [(i, (i + 1) % count) for i in range(count)])  11.1 us
    ppermute x6, starting transfers between devices, extended_2(): lax.ppermute(tail, axis, [(i, (i + 1) % count) for i in range(count)])  10.5 us
    ppermute x6, waiting for transfers between devices, extended_2(): lax.ppermute(head, axis, [((i + 1) % count, i) for i in range(count)])  9.49 us
  transfers between devices with their start and end apart: 12, of which 11 were waited for; matrix products, arithmetic and copies ran while one was open for 1% of the time, Pallas kernels for 0%

profile of v1, /device:TPU:21, one launch (start us, length us, event | category | flops | bytes accessed | tf_op | source)
XLA Modules:
  0.0 142.7 jit_solution(5915960308053739537)
XLA Ops:
  0.0 0.0 copy-start
  0.0 0.8 copy.5
  0.8 0.9 select_bitcast_fusion
  1.7 0.0 copy-done
  1.7 0.3 collective-permute-start
  2.0 1.2 collective-permute-start.1
  3.2 1.1 collective-permute-done
  4.4 0.2 collective-permute-done.1
  4.6 3.3 %collective-permute-start.2 = (f32[4,10,1,2,128]{4,3,2,1,0:T(2,128)S(1)}, f32[4,10,1,2,128]{4,3,2,1,0:T(2,128)S(1)}, u32[]{:S(2)}, u32[]{:S(2)}) collective-permute-start(f32[4,10,1,2,128]{4,3,2,1,0:T(2,128)S(1)} %get-tuple-element.9), channel_id=1, source_target_pairs={{0,4},{4,8},{8,12},{12,0},{1,5},{5,9},{9,13},{13,1},{2,6},{6,10},{... | collective-permute-start | bytes 122888 | tf_op jit(solution)/shard_map/ppermute | solution.py:178
  7.9 0.0 collective-permute-start.3
  7.9 1.1 collective-permute-done.2
  9.0 2.3 %collective-permute-done.3 = f32[4,10,1,2,128]{4,3,2,1,0:T(2,128)S(1)} collective-permute-done((f32[4,10,1,2,128]{4,3,2,1,0:T(2,128)S(1)}, f32[4,10,1,2,128]{4,3,2,1,0:T(2,128)S(1)}, u32[]{:S(2)}, u32[]{:S(2)}) %collective-permute-start.3) | collective-permute-done | bytes 40992 | tf_op jit(solution)/shard_map/ppermute | solution.py:180
  11.3 0.1 pad_maximum_fusion.2
  11.4 0.2 fusion
  11.6 1.3 collective-permute-start.4
  13.0 0.2 collective-permute-start.5
  13.2 5.6 %collective-permute-done.4 = f32[4,10,6,1,128]{4,3,2,1,0:T(1,128)S(1)} collective-permute-done((f32[4,10,6,1,128]{4,3,2,1,0:T(1,128)S(1)}, f32[4,10,6,1,128]{4,3,2,1,0:T(1,128)S(1)}, u32[]{:S(2)}, u32[]{:S(2)}) %collective-permute-start.4) | collective-permute-done | bytes 122912 | tf_op jit(solution)/shard_map/ppermute | solution.py:178
  18.7 0.0 collective-permute-done.5
  18.7 1.1 pad_maximum_fusion
  19.9 50.7 %shard_map.46 = f32[3,64,128]{2,1,0:T(8,128)} custom-call(f32[4,240,128]{2,1,0:T(8,128)} %bitcast.20, f32[3,64,128]{2,1,0:T(8,128)} %bitcast.13), custom_call_target="tpu_custom_call" | custom-call | tf_op jit(solution)/shard_map/pallas_call | solution.py:156
  70.6 0.0 copy-start.1
  70.6 0.0 copy-start.3
  70.6 0.9 broadcast_multiply_fusion.2
  71.5 0.0 copy-done.1
  71.6 0.0 copy-done.3
  71.6 0.0 copy-start.2
  71.6 1.3 collective-permute-start.6
  72.9 0.2 collective-permute-start.7
  73.2 1.4 collective-permute-done.6
  74.6 0.9 collective-permute-done.7
  75.5 2.9 %collective-permute-start.8 = (f32[3,10,1,2,128]{4,3,2,1,0:T(2,128)S(1)}, f32[3,10,1,2,128]{4,3,2,1,0:T(2,128)S(1)}, u32[]{:S(2)}, u32[]{:S(2)}) collective-permute-start(f32[3,10,1,2,128]{4,3,2,1,0:T(2,128)S(1)} %get-tuple-element.13), channel_id=1, source_target_pairs={{0,4},{4,8},{8,12},{12,0},{1,5},{5,9},{9,13},{13,1},{2,6},{6,10},{... | collective-permute-start | bytes 92168 | tf_op jit(solution)/shard_map/ppermute | solution.py:178
  78.5 0.0 collective-permute-start.9
  78.5 1.0 collective-permute-done.8
  79.5 2.3 %collective-permute-done.9 = f32[3,10,1,2,128]{4,3,2,1,0:T(2,128)S(1)} collective-permute-done((f32[3,10,1,2,128]{4,3,2,1,0:T(2,128)S(1)}, f32[3,10,1,2,128]{4,3,2,1,0:T(2,128)S(1)}, u32[]{:S(2)}, u32[]{:S(2)}) %collective-permute-start.9) | collective-permute-done | bytes 30752 | tf_op jit(solution)/shard_map/ppermute | solution.py:180
  81.8 0.1 pad_maximum_fusion.3
  81.9 0.1 fusion.1
  82.0 1.3 collective-permute-start.10
  83.4 0.2 collective-permute-start.11
  83.5 0.1 iota_compare_fusion
  83.6 0.9 slice.58
  84.5 0.9 collective-permute-done.10
  85.5 3.7 %collective-permute-done.11 = f32[3,10,6,1,128]{4,3,2,1,0:T(1,128)S(1)} collective-permute-done((f32[3,10,6,1,128]{4,3,2,1,0:T(1,128)S(1)}, f32[3,10,6,1,128]{4,3,2,1,0:T(1,128)S(1)}, u32[]{:S(2)}, u32[]{:S(2)}) %collective-permute-start.11) | collective-permute-done | bytes 92192 | tf_op jit(solution)/shard_map/ppermute | solution.py:180
  89.2 0.0 copy-done.2
  89.2 1.1 pad_maximum_fusion.1
  90.3 50.7 %shard_map.47 = f32[3,64,128]{2,1,0:T(8,128)} custom-call(f32[4,240,128]{2,1,0:T(8,128)} %bitcast.21, f32[3,64,128]{2,1,0:T(8,128)} %bitcast.19), custom_call_target="tpu_custom_call" | custom-call | tf_op jit(solution)/shard_map/pallas_call | solution.py:156
  141.0 0.9 broadcast_multiply_fusion
  141.9 0.8 add_select_fusion
  (5 shorter events, 0.1 us)
Async XLA Ops:
  0.0 1.7 %copy-start = (f32[3,8,4,2,128]{4,3,2,1,0:T(2,128)S(1)}, f32[3,8,4,2,128]{4,3,2,1,0:T(2,128)}, u32[]{:S(2)}) copy-start(f32[3,8,4,2,128]{4,3,2,1,0:T(2,128)} %param.4) | copy-start | bytes 294916
  1.7 2.7 %collective-permute-start = (f32[4,1,4,2,128]{4,3,2,1,0:T(2,128)S(1)}, f32[4,1,4,2,128]{4,3,2,1,0:T(2,128)S(1)}, u32[]{:S(2)}, u32[]{:S(2)}) collective-permute-start(f32[4,1,4,2,128]{4,3,2,1,0:T(2,128)S(1)} %get-tuple-element.11), channel_id=1, source_target_pairs={{0,16},{16,0},{1,17},{17,1},{2,18},{18,2},{3,19},{19,3},{4,20},{20... | collective-permute-start | bytes 49160 | tf_op jit(solution)/shard_map/ppermute | solution.py:178
  2.0 2.6 %collective-permute-start.1 = (f32[4,1,4,2,128]{4,3,2,1,0:T(2,128)S(1)}, f32[4,1,4,2,128]{4,3,2,1,0:T(2,128)S(1)}, u32[]{:S(2)}, u32[]{:S(2)}) collective-permute-start(f32[4,1,4,2,128]{4,3,2,1,0:T(2,128)S(1)} %get-tuple-element.12), channel_id=1, source_target_pairs={{16,0},{0,16},{17,1},{1,17},{18,2},{2,18},{19,3},{3,19},{20,4},{4,... | collective-permute-start | bytes 49160 | tf_op jit(solution)/shard_map/ppermute | solution.py:180
  4.6 4.4 %collective-permute-start.2 = (f32[4,10,1,2,128]{4,3,2,1,0:T(2,128)S(1)}, f32[4,10,1,2,128]{4,3,2,1,0:T(2,128)S(1)}, u32[]{:S(2)}, u32[]{:S(2)}) collective-permute-start(f32[4,10,1,2,128]{4,3,2,1,0:T(2,128)S(1)} %get-tuple-element.9), channel_id=1, source_target_pairs={{0,4},{4,8},{8,12},{12,0},{1,5},{5,9},{9,13},{13,1},{2,6},{6,10},{... | collective-permute-start | bytes 122888 | tf_op jit(solution)/shard_map/ppermute | solution.py:178
  7.9 3.4 %collective-permute-start.3 = (f32[4,10,1,2,128]{4,3,2,1,0:T(2,128)S(1)}, f32[4,10,1,2,128]{4,3,2,1,0:T(2,128)S(1)}, u32[]{:S(2)}, u32[]{:S(2)}) collective-permute-start(f32[4,10,1,2,128]{4,3,2,1,0:T(2,128)S(1)} %get-tuple-element.10), channel_id=1, source_target_pairs={{4,0},{8,4},{12,8},{0,12},{5,1},{9,5},{13,9},{1,13},{6,2},{10,6},{... | collective-permute-start | bytes 122888 | tf_op jit(solution)/shard_map/ppermute | solution.py:180
  11.6 7.1 %collective-permute-start.4 = (f32[4,10,6,1,128]{4,3,2,1,0:T(1,128)S(1)}, f32[4,10,6,1,128]{4,3,2,1,0:T(1,128)S(1)}, u32[]{:S(2)}, u32[]{:S(2)}) collective-permute-start(f32[4,10,6,1,128]{4,3,2,1,0:T(1,128)S(1)} %get-tuple-element.5), channel_id=1, source_target_pairs={{0,1},{1,2},{2,3},{3,0},{4,5},{5,6},{6,7},{7,4},{8,9},{9,10},{10,1... | collective-permute-start | bytes 368648 | tf_op jit(solution)/shard_map/ppermute | solution.py:178
  13.0 5.8 %collective-permute-start.5 = (f32[4,10,6,1,128]{4,3,2,1,0:T(1,128)S(1)}, f32[4,10,6,1,128]{4,3,2,1,0:T(1,128)S(1)}, u32[]{:S(2)}, u32[]{:S(2)}) collective-permute-start(f32[4,10,6,1,128]{4,3,2,1,0:T(1,128)S(1)} %get-tuple-element.6), channel_id=1, source_target_pairs={{1,0},{2,1},{3,2},{0,3},{5,4},{6,5},{7,6},{4,7},{9,8},{10,9},{11,1... | collective-permute-start | bytes 368648 | tf_op jit(solution)/shard_map/ppermute | solution.py:180
  70.6 1.0 copy-start.1
  70.6 1.0 copy-start.3
  71.6 17.6 %copy-start.2 = (f32[3,8,1,8,128]{4,3,2,1,0:T(8,128)}, f32[3,8,1,8,128]{4,3,2,1,0:T(8,128)S(1)}, u32[]{:S(2)}) copy-start(f32[3,8,1,8,128]{4,3,2,1,0:T(8,128)S(1)} %add_add_fusion) | copy-start | bytes 294916
  71.6 2.9 %collective-permute-start.6 = (f32[3,1,4,2,128]{4,3,2,1,0:T(2,128)S(1)}, f32[3,1,4,2,128]{4,3,2,1,0:T(2,128)S(1)}, u32[]{:S(2)}, u32[]{:S(2)}) collective-permute-start(f32[3,1,4,2,128]{4,3,2,1,0:T(2,128)S(1)} %get-tuple-element.17), channel_id=1, source_target_pairs={{0,16},{16,0},{1,17},{17,1},{2,18},{18,2},{3,19},{19,3},{4,20},{20... | collective-permute-start | bytes 36872 | tf_op jit(solution)/shard_map/ppermute | solution.py:178
  72.9 2.5 %collective-permute-start.7 = (f32[3,1,4,2,128]{4,3,2,1,0:T(2,128)S(1)}, f32[3,1,4,2,128]{4,3,2,1,0:T(2,128)S(1)}, u32[]{:S(2)}, u32[]{:S(2)}) collective-permute-start(f32[3,1,4,2,128]{4,3,2,1,0:T(2,128)S(1)} %get-tuple-element.18), channel_id=1, source_target_pairs={{16,0},{0,16},{17,1},{1,17},{18,2},{2,18},{19,3},{3,19},{20,4},{4,... | collective-permute-start | bytes 36872 | tf_op jit(solution)/shard_map/ppermute | solution.py:180
  75.5 4.0 %collective-permute-start.8 = (f32[3,10,1,2,128]{4,3,2,1,0:T(2,128)S(1)}, f32[3,10,1,2,128]{4,3,2,1,0:T(2,128)S(1)}, u32[]{:S(2)}, u32[]{:S(2)}) collective-permute-start(f32[3,10,1,2,128]{4,3,2,1,0:T(2,128)S(1)} %get-tuple-element.13), channel_id=1, source_target_pairs={{0,4},{4,8},{8,12},{12,0},{1,5},{5,9},{9,13},{13,1},{2,6},{6,10},{... | collective-permute-start | bytes 92168 | tf_op jit(solution)/shard_map/ppermute | solution.py:178
  78.5 3.3 %collective-permute-start.9 = (f32[3,10,1,2,128]{4,3,2,1,0:T(2,128)S(1)}, f32[3,10,1,2,128]{4,3,2,1,0:T(2,128)S(1)}, u32[]{:S(2)}, u32[]{:S(2)}) collective-permute-start(f32[3,10,1,2,128]{4,3,2,1,0:T(2,128)S(1)} %get-tuple-element.14), channel_id=1, source_target_pairs={{4,0},{8,4},{12,8},{0,12},{5,1},{9,5},{13,9},{1,13},{6,2},{10,6},{... | collective-permute-start | bytes 92168 | tf_op jit(solution)/shard_map/ppermute | solution.py:180
  82.0 3.5 %collective-permute-start.10 = (f32[3,10,6,1,128]{4,3,2,1,0:T(1,128)S(1)}, f32[3,10,6,1,128]{4,3,2,1,0:T(1,128)S(1)}, u32[]{:S(2)}, u32[]{:S(2)}) collective-permute-start(f32[3,10,6,1,128]{4,3,2,1,0:T(1,128)S(1)} %get-tuple-element.7), channel_id=1, source_target_pairs={{0,1},{1,2},{2,3},{3,0},{4,5},{5,6},{6,7},{7,4},{8,9},{9,10},{10,1... | collective-permute-start | bytes 276488 | tf_op jit(solution)/shard_map/ppermute | solution.py:178
  83.4 5.8 %collective-permute-start.11 = (f32[3,10,6,1,128]{4,3,2,1,0:T(1,128)S(1)}, f32[3,10,6,1,128]{4,3,2,1,0:T(1,128)S(1)}, u32[]{:S(2)}, u32[]{:S(2)}) collective-permute-start(f32[3,10,6,1,128]{4,3,2,1,0:T(1,128)S(1)} %get-tuple-element.8), channel_id=1, source_target_pairs={{1,0},{2,1},{3,2},{0,3},{5,4},{6,5},{7,6},{4,7},{9,8},{10,9},{11,1... | collective-permute-start | bytes 276488 | tf_op jit(solution)/shard_map/ppermute | solution.py:180
